TPU v7x, 32 devices: a whole 2x2x4 slice. The times are simulated.
32 devices in a mesh: seq: 8 (over z, x), feat: 4 (over y, core).
Axes of the slice: x: 2, y: 2, z: 4, core: 2. Of those that a mesh axis runs over, the one named last changes fastest.
Arguments:
- teacher_states: bfloat16 [4, 8192, 3584], P(None, 'seq', 'feat')
- student_states: bfloat16 [8192, 2304], P('seq'), may hold values from -6 to 6
- projection: bfloat16 [4, 2304, 3584], P(None, 'seq', 'feat'), may hold values from -0.125 to 0.125
- layer_pick: int32 [4], replicated, may hold values from 0 to 3, each once
- validity: int32 [8192], P('seq'), may hold values from 0 to 1, as said below
Outputs:
- whitened_error: bfloat16 [4, 8192, 3584], P(None, 'seq', 'feat')
- total_loss: float32 [], replicated
Inputs may be any that keep to these rules, and one draw needn't show every extreme that they name: `validity`: the positions form 2 sequences of 4096 positions each; in each sequence a prefix of 1024 positions or more is 1 and the rest is 0.
All inputs are finite; a program needn't handle non-finite values.
Results may differ from a plain program's by a relative error of at most 0.00045.
Values may be sent and summed in bfloat16 or wider, within the bound.
A program may use at most 128 MiB of HBM per device.

v0:
```python
import jax
import jax.numpy as jnp
from jax import lax
from jax.sharding import PartitionSpec as P

D = 3584
LAYERS = 4


epsilon = 1e-05


def shards(teacher_states, student_states, projection, layer_pick, validity):
    weighting = validity.astype(jnp.float32)
    local_count = jnp.sum(weighting)
    chosen = jnp.take(teacher_states, layer_pick, axis=0).astype(jnp.float32)
    masked = weighting[None, :, None]
    local_sums = jnp.sum(chosen * masked, axis=1)
    summed, counted = lax.psum((local_sums, local_count), "seq")
    average = summed / counted
    centred = chosen - average[:, None, :]
    squares = jnp.sum(masked * centred * centred, axis=1)
    variance = lax.psum(squares, "seq") / counted
    target = centred / jnp.sqrt(variance + epsilon)[:, None, :]
    predicted = jnp.einsum(
        "tr,lrd->ltd",
        student_states,
        lax.all_gather(projection, "seq", axis=1, tiled=True),
        preferred_element_type=jnp.float32,
    )
    residual = predicted - target
    whitened_error = (masked * residual).astype(jnp.bfloat16)
    partial_value = jnp.sum(masked * residual * residual)
    squared_total = lax.psum(partial_value, ("seq", "feat"))
    total_loss = squared_total / (counted * D * LAYERS)
    return (whitened_error, total_loss)


def solution(mesh):
    placed = (P(None, "seq", "feat"), P("seq", None), P(None, "seq", "feat"), P(), P("seq"))
    return jax.shard_map(
        shards, mesh=mesh, in_specs=placed, out_specs=(P(None, "seq", "feat"), P()), check_vma=False
    )
```

profile of v0, /device:TPU:0, one launch (start us, length us, event | category | flops | bytes accessed | tf_op | source)
XLA Modules:
  0.0 325.8 jit_solution(4154889889443646090)
XLA Ops:
  7.2 0.0 all-gather.2.cloned.1.call-start
  7.2 0.7 all-gather.2.cloned.1.call-update
  7.9 0.7 compare_select_fusion
  8.6 7.5 %gather_fusion = bf16[4,1024,896]{2,1,0:T(8,128)(2,1)} fusion(bf16[4,1024,896]{2,1,0:T(8,128)(2,1)} %param.5, s32[1024]{0:T(1024)S(1)} %pad_clamp_fusion), kind=kCustom, calls=%fused_computation | custom fusion | bytes 14680080 | tf_op jit(solution)/shard_map/jit(_take)/gather | solution.py:16
  16.1 0.0 copy-start
  16.1 0.0 copy-start.1
  16.1 11.4 %copy.8 = bf16[4,1024,896]{1,2,0:T(8,128)(2,1)} copy(bf16[4,1024,896]{2,1,0:T(8,128)(2,1)} %gather_fusion) | data formatting | bytes 14680064 | tf_op jit(solution)/shard_map/jit(_take)/gather | solution.py:16
  27.5 0.0 copy-done
  27.5 0.6 convert_reduce_fusion
  28.1 0.0 copy-done.1
  28.1 5.1 %fusion.2 = f32[4,896]{1,0:T(4,128)S(1)} fusion(f32[1024]{0:T(1024)S(1)} %convert_element_type.9, bf16[4,1024,896]{1,2,0:T(8,128)(2,1)} %copy.8, pred[4]{0:T(512)(128)(4,1)S(1)} %compare_and_fusion), kind=kLoop, calls=%fused_computation.8 | loop fusion | flops 14676480 | bytes 7358468 | tf_op jit(solution)/shard_map/reduce_sum | solution.py:18
  33.3 41.7 %all-reduce = (f32[4,896]{1,0:T(4,128)S(1)}, f32[]{:T(128)}) all-reduce(f32[4,896]{1,0:T(4,128)S(1)} %fusion.2, f32[]{:T(128)} %convert_reduce_fusion), channel_id=1, replica_groups=mesh['seq'=8,'feat'=4] {'seq'}, use_global_device_ids=true, to_apply=%region_1.2 | all-reduce | flops 3585 | bytes 28680 | tf_op jit(solution)/shard_map/psum | solution.py:19
  75.6 0.7 broadcast_divide_fusion
  76.3 5.9 %fusion.4 = f32[4,896]{1,0:T(4,128)S(1)} fusion(f32[4,896]{1,0:T(4,128)S(1)} %broadcast_divide_fusion, f32[1024]{0:T(1024)S(1)} %convert_element_type.9, bf16[4,1024,896]{1,2,0:T(8,128)(2,1)} %copy.8, pred[4]{0:T(512)(128)(4,1)S(1)} %compare_and_fusion), kind=kLoop, calls=%fused_computation.10 | loop fusion | flops 22016512 | bytes 7372804 | tf_op jit(solution)/shard_map/reduce_sum | solution.py:22
  82.2 34.8 %psum.30 = f32[4,896]{1,0:T(4,128)S(1)} all-reduce(f32[4,896]{1,0:T(4,128)S(1)} %fusion.4), channel_id=1, replica_groups=mesh['seq'=8,'feat'=4] {'seq'}, use_global_device_ids=true, to_apply=%region_5.6 | all-reduce | flops 3584 | bytes 28672 | tf_op jit(solution)/shard_map/psum | solution.py:23
  117.0 0.7 add_sqrt_fusion
  117.6 120.5 %all-gather.2.cloned.1.call-done = bf16[4,2304,896]{2,1,0:T(8,128)(2,1)} async-done(((bf16[4,288,896]{2,1,0:T(8,128)(2,1)}), bf16[4,2304,896]{2,1,0:T(8,128)(2,1)}) %all-gather.2.cloned.1.call-update) | async-done | bytes 16515088 | tf_op jit(solution)/shard_map/all_gather | solution.py:28
  238.1 29.6 %fusion.3 = (f32[]{:T(128)}, bf16[4,1024,896]{1,2,0:T(8,128)(2,1)}) fusion(f32[1024]{0:T(1024)S(1)} %convert_element_type.9, f32[4,896]{1,0:T(4,128)S(1)} %add_sqrt_fusion, f32[4,896]{1,0:T(4,128)S(1)} %broadcast_divide_fusion, bf16[4,1024,896]{1,2,0:T(8,128)(2,1)} %copy.8, pred[4]{0:T(512)(128)(4,1)S(1)} %compare_and_fusion, ...), kind=kOutput, calls=%fused_computation.9 | convolution fusion | flops 16944463872 | bytes 35946504 | tf_op jit(solution)/shard_map/tr,lrd->ltd/dot_general | solution.py:25
  267.7 38.6 %psum.31 = f32[]{:T(128)} all-reduce(f32[]{:T(128)} %get-tuple-element.8), channel_id=1, replica_groups=mesh['seq'=8,'feat'=4] {'seq','feat'}, use_global_device_ids=true, to_apply=%region_7.8 | all-reduce | flops 1 | bytes 8 | tf_op jit(solution)/shard_map/psum | solution.py:34
  306.3 10.9 %copy.9 = bf16[4,1024,896]{2,1,0:T(8,128)(2,1)} copy(bf16[4,1024,896]{1,2,0:T(8,128)(2,1)} %get-tuple-element.9) | data formatting | bytes 14680064
  (3 shorter events, 0.0 us)
Async XLA Ops:
  7.2 230.9 %all-gather.2.cloned.1.call-start = ((), (), s32[]{:S(2)}) async-start(), calls=%async_computation | async-start | bytes 18579456 | tf_op jit(solution)/shard_map/all_gather | solution.py:28
  16.1 11.4 %copy-start = (s32[1024]{0:T(1024)S(1)}, s32[1024]{0:T(1024)}, u32[]{:S(2)}) copy-start(s32[1024]{0:T(1024)} %param.9) | copy-start | bytes 12292
  16.1 12.0 %copy-start.1 = (s32[4]{0:T(128)S(1)}, s32[4]{0:T(128)}, u32[]{:S(2)}) copy-start(s32[4]{0:T(128)} %param.8) | copy-start | bytes 52
Sparse Core Ops, SparseCore 0:
  10.2 227.8 all-gather.1
where the time goes:
time: 327 us; the launch traced here: 326 us
  waiting for transfers between devices  121 us (37%)
  blocking collectives  115 us (35%)
  local copies, waits for them, and re-layouts  29.9 us (9%)
  matrix products  29.6 us (9%)
  between operations  16.5 us (5%)
  other arithmetic  13.6 us (4%)
    all_gather x1, waiting for transfers between devices, shards(): lax.all_gather(projection, 'seq', axis=1, tiled=True)  120 us
    psum x1, blocking collectives, shards(): summed, counted = lax.psum((local_sums, local_count), 'seq')  41.7 us
    psum x1, blocking collectives, shards(): squared_total = lax.psum(partial_value, ('seq', 'feat'))  38.6 us
    psum x1, blocking collectives, shards(): variance = lax.psum(squares, 'seq') / counted  34.8 us
    dot_general x1, matrix products, shards(): jnp.einsum('tr,lrd->ltd', student_states, lax.all_gather(projection, 'seq...  29.6 us
    gather x2, local copies, waits for them, and re-layouts, shards(): chosen = jnp.take(teacher_states, layer_pick, axis=0).astype(jnp.float32)  18.9 us
    unnamed x5, local copies, waits for them, and re-layouts  10.9 us
  transfers between devices with their start and end apart: 1, of which 1 were waited for; matrix products, arithmetic and copies ran while one was open for 10% of the time, Pallas kernels for 0%

commit v1 on v0

v1 whole, which is shorter than its diff:
```python
import functools

import jax
import jax.numpy as jnp
from jax import lax
from jax.experimental import pallas as pl
from jax.experimental.pallas import tpu as pltpu
from jax.sharding import PartitionSpec as P

epsilon = 1e-05
WIDE = 2
F32 = jnp.float32


def plain(teacher_states, student_states, projection, layer_pick, validity, *, feats):
    layers = projection.shape[0]
    width = projection.shape[2] * feats
    weighting = validity.astype(F32)
    chosen = jnp.take(teacher_states, layer_pick, axis=0).astype(F32)
    masked = weighting[None, :, None]
    summed, counted = lax.psum((jnp.sum(chosen * masked, axis=1), jnp.sum(weighting)), "seq")
    centred = chosen - (summed / counted)[:, None, :]
    variance = lax.psum(jnp.sum(masked * centred * centred, axis=1), "seq") / counted
    target = centred / jnp.sqrt(variance + epsilon)[:, None, :]
    predicted = jnp.einsum(
        "tr,lrd->ltd",
        student_states,
        lax.all_gather(projection, "seq", axis=1, tiled=True),
        preferred_element_type=F32,
    )
    residual = predicted - target
    squared_total = lax.psum(jnp.sum(masked * residual * residual), ("seq", "feat"))
    return (masked * residual).astype(jnp.bfloat16), squared_total / (counted * width * layers)


def kernel(
    ndev, feats, tile,
    pick, weight, teacher, student, proj, out, loss,
    W, S, T, O, mine, stats, centre, inv, counted, total,
    load_sem, send_sem, recv_sem, stat_send, stat_recv, out_sem,
):
    layers, rows, cols = proj.shape
    tokens = student.shape[0]
    deep = ndev // WIDE
    half = rows // 2
    me = lax.axis_index("seq")
    z, x = me // WIDE, me % WIDE
    other = 1 - x
    pair = z + 1 - 2 * (z % 2)
    reps = cols // 128

    def piece(block, layer, start=0, size=rows):
        return W.at[layer, pl.ds(pl.multiple_of(block * rows + start, 16), size), :]

    def send(src, dst, to, layer, slot, block, part):
        return pltpu.make_async_remote_copy(
            src_ref=src, dst_ref=dst, send_sem=send_sem.at[layer, slot],
            recv_sem=recv_sem.at[layer, block, part],
            device_id={"seq": to}, device_id_type=pl.DeviceIdType.MESH,
        )

    def landed(block, layer, part, start=0, size=rows):
        ref = piece(block, layer, start, size)
        send(ref, ref, me, layer, 0, block, part).wait_recv()

    up, down, across = me + WIDE, me - WIDE, z * WIDE + other
    has_up, has_down = z + 1 < deep, z > 0

    def own(layer, act):
        for slot, to, ok in ((2, across, None), (0, up, has_up), (1, down, has_down)):
            def go(slot=slot, to=to):
                act(send(proj.at[layer], piece(me, layer), to, layer, slot, me, 0))
            go() if ok is None else pl.when(ok)(go)

    def forward(layer, d, act, arrive):
        for sign, to, onward in ((-1, up, has_up), (1, down, has_down)):
            b = z + sign * d
            @pl.when((b >= 0) & (b < deep))
            def _():
                block = b * WIDE + x
                if arrive:
                    landed(block, layer, 0)
                @pl.when(onward)
                def _():
                    ref = piece(block, layer)
                    act(send(ref, ref, to, layer, 3 + b, block, 0))
                @pl.when(b == pair)
                def _():
                    ref = piece(block, layer, 0, half)
                    act(send(ref, ref, across, layer, 3 + deep + b, block, 0))
                @pl.when(b != pair)
                def _():
                    ref = piece(block, layer)
                    act(send(ref, ref, across, layer, 3 + deep + b, block, 0))

    def halves(layer, act, arrive):
        if arrive:
            landed(across, layer, 0)
        ref = piece(across, layer, half, half)
        act(send(ref, ref, pair * WIDE + x, layer, 3 + 2 * deep, across, 1))

    start = lambda c: c.start()
    finish = lambda c: c.wait_send()

    own(0, start)
    own(1, start)
    get_t = pltpu.make_async_copy(teacher, T, load_sem.at[0])
    get_s = pltpu.make_async_copy(student, S, load_sem.at[1])
    get_p = pltpu.make_async_copy(
        proj, W.at[:, pl.ds(pl.multiple_of(me * rows, 16), rows), :], load_sem.at[2]
    )
    get_t.start()
    get_s.start()
    get_p.start()

    chunk = 64
    steps = tokens // chunk

    def spread(at, size):
        w = weight[pl.ds(pl.multiple_of(at, 8), size), :]
        return jnp.concatenate([w] * reps, axis=1)

    def fold(v):
        return jnp.sum(v.reshape(v.shape[0] // 8, 8, cols), axis=0)

    zero = jnp.zeros((8, cols), F32)
    count = jnp.sum(
        lax.fori_loop(
            0, steps,
            lambda i, a: a + jnp.sum(weight[pl.ds(pl.multiple_of(i * chunk, 8), chunk), :].reshape(chunk // 8, 8, 128), axis=0),
            jnp.zeros((8, 128), F32),
        ), axis=0, keepdims=True)
    counts = jnp.concatenate([count] * reps, axis=1)
    get_t.wait()
    means, spreads = [], []
    for s in range(layers):
        def add(i, a):
            c = T[s, pl.ds(pl.multiple_of(i * chunk, 16), chunk), :].astype(F32)
            return a + fold(c * spread(i * chunk, chunk))
        average = jnp.sum(lax.fori_loop(0, steps, add, zero), axis=0, keepdims=True) / jnp.maximum(counts, 1.0)

        def square(i, a):
            c = T[s, pl.ds(pl.multiple_of(i * chunk, 16), chunk), :].astype(F32) - average
            return a + fold(c * c * spread(i * chunk, chunk))
        squares = jnp.sum(lax.fori_loop(0, steps, square, zero), axis=0, keepdims=True)
        means.append(average)
        spreads.append(squares)
    mine[:, :cols] = jnp.concatenate(means + spreads, axis=0)
    mine[:, cols:] = jnp.broadcast_to(count, (2 * layers, 128))

    def stat(k):
        return pltpu.make_async_remote_copy(
            src_ref=mine, dst_ref=stats.at[k], send_sem=stat_send.at[k], recv_sem=stat_recv.at[k],
            device_id={"seq": (me + k) % ndev}, device_id_type=pl.DeviceIdType.MESH,
        )

    for k in range(1, ndev):
        stat(k).start()
    stats[0] = mine[...]
    total[...] = jnp.zeros_like(total)

    def combine():
        for k in range(1, ndev):
            stat(k).wait_recv()
        held = [stats[k] for k in range(ndev)]
        weights = [jnp.concatenate([v[0:1, cols:]] * reps, axis=1) for v in held]
        n = sum(weights[1:], weights[0])
        counted[...] = jnp.broadcast_to(n, (8, cols))
        for s in range(layers):
            average = jnp.zeros((1, cols), F32)
            for nk, v in zip(weights, held):
                average = average + nk * v[s : s + 1, :cols]
            average = average / n
            squares = jnp.zeros((1, cols), F32)
            for nk, v in zip(weights, held):
                off = v[s : s + 1, :cols] - average
                squares = squares + v[layers + s : layers + s + 1, :cols] + nk * off * off
            centre[s] = jnp.broadcast_to(average, (8, cols))
            inv[s] = jnp.broadcast_to(1.0 / jnp.sqrt(squares / n + epsilon), (8, cols))

    def write(layer, m):
        at = pl.ds(pl.multiple_of(m * tile, 16), tile)
        return pltpu.make_async_copy(O.at[layer, at, :], out.at[layer, at, :], out_sem.at[layer, m])

    def compute(layer):
        for b in range(deep):
            block = b * WIDE + other
            @pl.when((b != z) & (b != pair))
            def _():
                landed(block, layer, 0)
        block = pair * WIDE + other
        landed(block, layer, 0, 0, half)
        landed(block, layer, 1, half, half)
        which = pick[layer]
        average = centre[which][0:1]
        inverse = inv[which][0:1]

        def body(m, c):
            at = pl.ds(pl.multiple_of(m * tile, 16), tile)
            predicted = jnp.dot(S[at, :], W[layer], preferred_element_type=F32)
            target = (T[which, at, :].astype(F32) - average) * inverse
            residual = predicted - target
            w = spread(m * tile, tile) * residual
            O[layer, at, :] = w.astype(O.dtype)
            total[...] += fold(w * residual)
            write(layer, m).start()
            return c
        lax.fori_loop(0, tokens // tile, body, 0)

    def phase(p, c):
        @pl.when(p < layers)
        def _():
            for d in range(1, deep):
                forward(p, d, start, True)
        @pl.when(p + 2 < layers)
        def _():
            own(p + 2, start)
            halves(p, start, True)
        @pl.when(p == layers - 1)
        def _():
            halves(layers - 2, start, True)
            halves(layers - 1, start, True)
        @pl.when(p == 1)
        def _():
            combine()
            get_s.wait()
            get_p.wait()
        @pl.when(p > 0)
        def _():
            compute(p - 1)
        return c
    lax.fori_loop(0, layers + 1, phase, 0)

    loss[0, 0] = jnp.sum(total[...] / (counted[...] * F32(cols * feats * layers)))

    def drain(layer, c):
        own(layer, finish)
        for d in range(1, deep):
            forward(layer, d, finish, False)
        halves(layer, finish, False)
        for m in range(tokens // tile):
            write(layer, m).wait()
        return c
    lax.fori_loop(0, layers, drain, 0)
    for k in range(1, ndev):
        stat(k).wait_send()


def fused(teacher_states, student_states, projection, layer_pick, validity, *, ndev, feats, tile):
    layers, rows, cols = projection.shape
    tokens, depth = student_states.shape
    deep = ndev // WIDE
    weight = jnp.broadcast_to(validity.astype(F32)[:, None], (tokens, 128))
    anywhere = pl.BlockSpec(memory_space=pl.ANY)
    smem = pl.BlockSpec(memory_space=pltpu.SMEM)
    bf16 = jnp.bfloat16
    error, partial = pl.pallas_call(
        functools.partial(kernel, ndev, feats, tile),
        out_shape=(
            jax.ShapeDtypeStruct((layers, tokens, cols), bf16),
            jax.ShapeDtypeStruct((1, 1), F32),
        ),
        in_specs=[smem, pl.BlockSpec(memory_space=pltpu.VMEM), anywhere, anywhere, anywhere],
        out_specs=(anywhere, smem),
        scratch_shapes=[
            pltpu.VMEM((layers, rows * ndev, cols), bf16),
            pltpu.VMEM((tokens, depth), bf16),
            pltpu.VMEM((layers, tokens, cols), bf16),
            pltpu.VMEM((layers, tokens, cols), bf16),
            pltpu.VMEM((2 * layers, cols + 128), F32),
            pltpu.VMEM((ndev, 2 * layers, cols + 128), F32),
            pltpu.VMEM((layers, 8, cols), F32),
            pltpu.VMEM((layers, 8, cols), F32),
            pltpu.VMEM((8, cols), F32),
            pltpu.VMEM((8, cols), F32),
            pltpu.SemaphoreType.DMA((3,)),
            pltpu.SemaphoreType.DMA((layers, 4 + 2 * deep)),
            pltpu.SemaphoreType.DMA((layers, ndev, 2)),
            pltpu.SemaphoreType.DMA((ndev,)),
            pltpu.SemaphoreType.DMA((ndev,)),
            pltpu.SemaphoreType.DMA((layers, tokens // tile)),
        ],
        compiler_params=pltpu.CompilerParams(
            has_side_effects=True, vmem_limit_bytes=67043328
        ),
        name="gather_whiten",
    )(layer_pick, weight, teacher_states, student_states, projection)
    return error, lax.psum(partial[0, 0], ("seq", "feat"))


def solution(mesh):
    ndev, feats = mesh.shape["seq"], mesh.shape["feat"]
    tile = 256
    placed = (P(None, "seq", "feat"), P("seq", None), P(None, "seq", "feat"), P(), P("seq"))

    def step(teacher_states, student_states, projection, layer_pick, validity):
        layers, rows, cols = projection.shape
        tokens = student_states.shape[0]
        kept = 2 * (rows * ndev * cols * layers + tokens * rows * ndev + 2 * layers * tokens * cols)
        fits = kept < (48 << 20) and ndev % (2 * WIDE) == 0 and layers >= 2
        if fits and rows % 32 == 0 and cols % 128 == 0 and tokens % tile == 0:
            run = functools.partial(fused, ndev=ndev, feats=feats, tile=tile)
        else:
            run = functools.partial(plain, feats=feats)
        return run(teacher_states, student_states, projection, layer_pick, validity)

    return jax.shard_map(
        step, mesh=mesh, in_specs=placed, out_specs=(P(None, "seq", "feat"), P()), check_vma=False
    )
```

time: 327 us -> 236 us (0.72)
  Pallas kernels: 0 us -> 189 us
  waiting for transfers between devices: 121 us -> 0 us
  blocking collectives: 115 us -> 37.1 us
  matrix products: 29.6 us -> 0 us
  local copies, waits for them, and re-layouts: 29.9 us -> 7.71 us
  between operations: 16.5 us -> 0.64 us
  other arithmetic: 13.6 us -> 0.69 us
    pallas_call x0 -> x1, Pallas kernels: none -> 189 us  [fused(): pl.pallas_call(functools.partial(kernel, ndev, feats, tile), out_shape=(j...]
    all_gather x1 -> x0, waiting for transfers between devices: 120 us -> none  [shards(): lax.all_gather(projection, 'seq', axis=1, tiled=True)]
    psum x3 -> x1, blocking collectives: 115 us -> 37.1 us  [fused(): return (error, lax.psum(partial[0, 0], ('seq', 'feat')))]
    dot_general x1 -> x0, matrix products: 29.6 us -> none  [shards(): jnp.einsum('tr,lrd->ltd', student_states, lax.all_gather(projection, 'seq...]
    gather x2 -> x0, local copies, waits for them, and re-layouts: 18.9 us -> none  [shards(): chosen = jnp.take(teacher_states, layer_pick, axis=0).astype(jnp.float32)]
    reduce_sum x3 -> x0, other arithmetic: 11.6 us -> none  [the longest x1 5.89 us: shards(): squares = jnp.sum(masked * centred * centred, axis=1)]
    unnamed x5 -> x1, local copies, waits for them, and re-layouts: 10.9 us -> 6.72 us
  transfers between devices with their start and end apart: 1 -> 0, of which waited for: 1 -> 0; matrix products, arithmetic and copies ran while one was open for 10% -> 0% of each run, Pallas kernels for 0% -> 0%
where the time goes in v1:
time: 236 us; the launch traced here: 235 us
  Pallas kernels  189 us (80%)
  blocking collectives  37.1 us (16%)
  local copies, waits for them, and re-layouts  7.71 us (3%)
    pallas_call x1, Pallas kernels, fused(): pl.pallas_call(functools.partial(kernel, ndev, feats, tile), out_shape=(j...  189 us
    psum x1, blocking collectives, fused(): return (error, lax.psum(partial[0, 0], ('seq', 'feat')))  37.1 us
    unnamed x1, local copies, waits for them, and re-layouts  6.72 us

profile of v1, /device:TPU:0, one launch (start us, length us, event | category | flops | bytes accessed | tf_op | source)
XLA Modules:
  0.0 234.9 jit_solution(2183165114898646768)
XLA Ops:
  0.6 0.7 convert_element_type.3
  1.3 1.0 broadcast_in_dim.2.weight
  2.3 188.7 %gather_whiten.1 = (bf16[4,1024,896]{2,1,0:T(8,128)(2,1)}, f32[1,1]{1,0:T(1,128)}) custom-call(s32[4]{0:T(128)} %pick.1, f32[1024,128]{1,0:T(8,128)} %broadcast_in_dim.2.weight, bf16[4,1024,896]{2,1,0:T(8,128)(2,1)} %teacher.1, bf16[1024,2304]{1,0:T(8,128)(2,1)} %student.1, bf16[4,288,896]{2,1,0:T(8,128)(2,1)} %proj.1), custom_call_target="tpu_custom_call" | custom-call | tf_op jit(solution)/shard_map/gather_whiten/pallas_call | solution.py:257
  191.0 37.1 %psum.7 = f32[]{:T(128)} all-reduce(f32[]{:T(128)} %bitcast), channel_id=1, replica_groups=mesh['seq'=8,'feat'=4] {'seq','feat'}, use_global_device_ids=true, to_apply=%region_0.0 | all-reduce | flops 1 | bytes 8 | tf_op jit(solution)/shard_map/psum | solution.py:288
  228.2 6.7 %copy.8 = bf16[4,1024,896]{2,1,0:T(8,128)(2,1)} copy(bf16[4,1024,896]{2,1,0:T(8,128)(2,1)} %get-tuple-element.8) | data formatting | bytes 14680064

commit v2 on v1

--- a/solution.py
+++ b/solution.py
@@ -36,8 +36,8 @@
 def kernel(
     ndev, feats, tile,
     pick, weight, teacher, student, proj, out, loss,
-    W, S, T, O, mine, stats, centre, inv, counted, total,
-    load_sem, send_sem, recv_sem, stat_send, stat_recv, out_sem,
+    W, S, T, O, mine, stats, centre, inv, counted, total, part,
+    load_sem, send_sem, recv_sem, stat_send, stat_recv, part_send, part_recv, out_sem,
 ):
     layers, rows, cols = proj.shape
     tokens = student.shape[0]
@@ -102,8 +102,8 @@
     start = lambda c: c.start()
     finish = lambda c: c.wait_send()
 
-    own(0, start)
-    own(1, start)
+    for l in range(layers):
+        own(l, start)
     get_t = pltpu.make_async_copy(teacher, T, load_sem.at[0])
     get_s = pltpu.make_async_copy(student, S, load_sem.at[1])
     get_p = pltpu.make_async_copy(
@@ -207,31 +207,58 @@
             return c
         lax.fori_loop(0, tokens // tile, body, 0)
 
+    last = deep - 1
+    for d in range(1, last):
+        def near(l, c, d=d):
+            forward(l, d, start, True)
+            if d == last - 1:
+                @pl.when(l < layers - 2)
+                def _():
+                    halves(l, start, True)
+                @pl.when(l == layers - 1)
+                def _():
+                    halves(layers - 2, start, True)
+                    halves(layers - 1, start, True)
+            return c
+        lax.fori_loop(0, layers, near, 0)
+    combine()
+    get_s.wait()
+    get_p.wait()
+
     def phase(p, c):
         @pl.when(p < layers)
         def _():
-            for d in range(1, deep):
-                forward(p, d, start, True)
-        @pl.when(p + 2 < layers)
-        def _():
-            own(p + 2, start)
-            halves(p, start, True)
-        @pl.when(p == layers - 1)
-        def _():
-            halves(layers - 2, start, True)
-            halves(layers - 1, start, True)
-        @pl.when(p == 1)
-        def _():
-            combine()
-            get_s.wait()
-            get_p.wait()
+            forward(p, last, start, True)
         @pl.when(p > 0)
         def _():
             compute(p - 1)
         return c
     lax.fori_loop(0, layers + 1, phase, 0)
 
-    loss[0, 0] = jnp.sum(total[...] / (counted[...] * F32(cols * feats * layers)))
+    share = total[...] / (counted[...] * F32(cols * feats * layers))
+    part[0] = sum(share[:, i * 128 : i * 128 + 128] for i in range(reps))
+
+    def gossip(axis, k, size, index, first):
+        return pltpu.make_async_remote_copy(
+            src_ref=part.at[first], dst_ref=part.at[first + k],
+            send_sem=part_send.at[first + k], recv_sem=part_recv.at[first + k],
+            device_id={axis: (index + k) % size}, device_id_type=pl.DeviceIdType.MESH,
+        )
+
+    def meet(axis, size, index, first):
+        copies = [gossip(axis, k, size, index, first) for k in range(1, size)]
+        for c in copies:
+            c.start()
+        for c in copies:
+            c.wait_recv()
+        return copies, sum(part[first + k] for k in range(size))
+
+    sent, value = meet("feat", feats, lax.axis_index("feat"), 0)
+    part[feats] = value
+    more, value = meet("seq", ndev, me, feats)
+    loss[0, 0] = jnp.sum(value)
+    for c in sent + more:
+        c.wait_send()
 
     def drain(layer, c):
         own(layer, finish)
@@ -273,11 +300,14 @@
             pltpu.VMEM((layers, 8, cols), F32),
             pltpu.VMEM((8, cols), F32),
             pltpu.VMEM((8, cols), F32),
+            pltpu.VMEM((feats + ndev, 8, 128), F32),
             pltpu.SemaphoreType.DMA((3,)),
             pltpu.SemaphoreType.DMA((layers, 4 + 2 * deep)),
             pltpu.SemaphoreType.DMA((layers, ndev, 2)),
             pltpu.SemaphoreType.DMA((ndev,)),
             pltpu.SemaphoreType.DMA((ndev,)),
+            pltpu.SemaphoreType.DMA((feats + ndev,)),
+            pltpu.SemaphoreType.DMA((feats + ndev,)),
             pltpu.SemaphoreType.DMA((layers, tokens // tile)),
         ],
         compiler_params=pltpu.CompilerParams(
@@ -285,7 +315,7 @@
         ),
         name="gather_whiten",
     )(layer_pick, weight, teacher_states, student_states, projection)
-    return error, lax.psum(partial[0, 0], ("seq", "feat"))
+    return error, partial[0, 0]
 
 
 def solution(mesh):
@@ -297,7 +327,7 @@
         layers, rows, cols = projection.shape
         tokens = student_states.shape[0]
         kept = 2 * (rows * ndev * cols * layers + tokens * rows * ndev + 2 * layers * tokens * cols)
-        fits = kept < (48 << 20) and ndev % (2 * WIDE) == 0 and layers >= 2
+        fits = kept < (48 << 20) and ndev % (2 * WIDE) == 0 and ndev > 2 * WIDE and layers >= 2
         if fits and rows % 32 == 0 and cols % 128 == 0 and tokens % tile == 0:
             run = functools.partial(fused, ndev=ndev, feats=feats, tile=tile)
         else:

time: 236 us -> 198 us (0.84)
  blocking collectives: 37.1 us -> 0 us
    psum x1 -> x0, blocking collectives: 37.1 us -> none  [fused(): return (error, lax.psum(partial[0, 0], ('seq', 'feat')))]
where the time goes in v2:
time: 198 us
  Pallas kernels  187 us (94%)
  local copies, waits for them, and re-layouts  7.71 us (4%)
  between operations  2.34 us (1%)
    pallas_call x1, Pallas kernels, fused(): pl.pallas_call(functools.partial(kernel, ndev, feats, tile), out_shape=(j...  187 us
    unnamed x1, local copies, waits for them, and re-layouts  6.72 us

profile of v2, /device:TPU:0, one launch (start us, length us, event | category | flops | bytes accessed | tf_op | source)
XLA Modules:
  0.0 198.2 jit_solution(14366505961112612706)
XLA Ops:
  0.6 0.7 convert_element_type.3
  1.3 1.0 broadcast_in_dim.2.weight
  2.3 187.4 %gather_whiten.1 = (bf16[4,1024,896]{2,1,0:T(8,128)(2,1)}, f32[1,1]{1,0:T(1,128)}) custom-call(s32[4]{0:T(128)} %pick.1, f32[1024,128]{1,0:T(8,128)} %broadcast_in_dim.2.weight, bf16[4,1024,896]{2,1,0:T(8,128)(2,1)} %teacher.1, bf16[1024,2304]{1,0:T(8,128)(2,1)} %student.1, bf16[4,288,896]{2,1,0:T(8,128)(2,1)} %proj.1), custom_call_target="tpu_custom_call" | custom-call | tf_op jit(solution)/shard_map/gather_whiten/pallas_call | solution.py:284
  189.7 6.7 %copy.9 = bf16[4,1024,896]{2,1,0:T(8,128)(2,1)} copy(bf16[4,1024,896]{2,1,0:T(8,128)(2,1)} %get-tuple-element.8) | data formatting | bytes 14680064
